TPU v7x, 256 devices: a 4x2x16 block of a 4x16x16 slice. The times are simulated.
256 devices in a mesh: group: 2 (over y), expert: 32 (over z, core), tensor: 4 (over x).
Axes of the slice: x: 4, y: 2, z: 16, core: 2. Of those that a mesh axis runs over, the one named last changes fastest.
The devices are a block of a 4x16x16 slice.
Arguments:
- tokens: bfloat16 [16384, 4096], P(('group', 'expert', 'tensor')), parts along dimension 0, may hold values from -6 to 6
- cotangent: bfloat16 [16384, 4096], P(('group', 'expert', 'tensor')), parts along dimension 0, may hold values from -6 to 6
- expert_ids: int32 [16384, 2], P(('group', 'expert', 'tensor')), parts along dimension 0, may hold values from 0 to 31, all different within a row
- gate_wts: float32 [16384, 2], P(('group', 'expert', 'tensor')), parts along dimension 0, may hold values from 0.2 to 1
- w_gate: bfloat16 [32, 4096, 256], P('expert', 'tensor'), may hold values from -0.09375 to 0.09375
- w_up: bfloat16 [32, 4096, 256], P('expert', 'tensor'), may hold values from -0.09375 to 0.09375
- w_down: bfloat16 [32, 256, 4096], P('expert', 'tensor'), may hold values from -0.375 to 0.375
Outputs:
- input_grad: bfloat16 [16384, 4096], P(('group', 'expert', 'tensor')), parts along dimension 0
- grad_gate: bfloat16 [64, 4096, 256], P(('group', 'expert'), 'tensor'), parts along dimension 0
- grad_up: bfloat16 [64, 4096, 256], P(('group', 'expert'), 'tensor'), parts along dimension 0
- grad_down: bfloat16 [64, 256, 4096], P(('group', 'expert'), 'tensor'), parts along dimension 0
There are 2 independent parts, one for each index of `group`. A program takes and returns all parts, laid end to end along the dimension named above; an argument that names none is the same for every part. Nothing has to cross between parts.
Inputs may be any that keep to these rules, and one draw needn't show every extreme that they name: `expert_ids`: the two ids of a token differ.
All inputs are finite; a program needn't handle non-finite values.
Results may differ from a plain program's by a relative error of at most 0.009.
Values may be sent and summed in bfloat16 or wider, within the bound.
A program may use at most 64 MiB of HBM per device.

v0:
```python
import jax
import jax.numpy as jnp
from jax import lax
from jax.sharding import PartitionSpec as P


def contract_last(left, right):
    return lax.dot_general(
        left, right, (((1,), (1,)), ((), ())), preferred_element_type=jnp.float32
    )


def contract_first(left, right):
    return lax.dot_general(
        left, right, (((0,), (0,)), ((), ())), preferred_element_type=jnp.float32
    )


def local(tokens, cotangent, expert_ids, gate_wts, w_gate, w_up, w_down):
    tok_rows, model_width = tokens.shape
    experts = lax.axis_size("expert")
    capacity = 2 * tok_rows // experts
    slots_all = experts * capacity
    zero_half = jnp.zeros((), jnp.bfloat16)
    flat_ids = expert_ids.reshape(-1)
    onehot = (flat_ids[:, None] == jnp.arange(experts, dtype=jnp.int32)[None, :]).astype(jnp.int32)
    positions = jnp.sum(onehot * (jnp.cumsum(onehot, axis=0) - 1), axis=1)
    retained = positions < capacity
    target = jnp.where(retained, flat_ids * capacity + positions, slots_all)
    anchor = (
        jnp.full((slots_all,), -1, jnp.int32)
        .at[target]
        .set(jnp.arange(2 * tok_rows, dtype=jnp.int32), mode="drop")
    )
    populated_rows = anchor >= 0
    picked = jnp.maximum(anchor, 0)
    tok_index = picked // 2
    send_rows = jnp.where(populated_rows[:, None], tokens[tok_index], zero_half)
    gate_scale = gate_wts.reshape(-1)[picked]
    scaled = (gate_scale[:, None] * cotangent[tok_index].astype(jnp.float32)).astype(jnp.bfloat16)
    send_cot = jnp.where(populated_rows[:, None], scaled, zero_half)
    recv_rows, recv_cot = (
        lax.all_to_all(
            send_rows.reshape(experts, capacity, model_width),
            "expert",
            split_axis=0,
            concat_axis=0,
            tiled=True,
        ),
        lax.all_to_all(
            send_cot.reshape(experts, capacity, model_width),
            "expert",
            split_axis=0,
            concat_axis=0,
            tiled=True,
        ),
    )
    rows_in = recv_rows.reshape(slots_all, model_width)
    cot_in = recv_cot.reshape(slots_all, model_width)
    gate_shard = w_gate[0]
    up_shard = w_up[0]
    down_shard = w_down[0]
    hidden_width = gate_shard.shape[1]
    full_gate, full_up, complete_down_weight = (
        lax.all_gather(gate_shard, "tensor", axis=0, tiled=True),
        lax.all_gather(up_shard, "tensor", axis=0, tiled=True),
        lax.all_gather(down_shard, "tensor", axis=0, tiled=True),
    )
    pre_gate = jnp.dot(rows_in, full_gate, preferred_element_type=jnp.float32)
    pre_up = jnp.dot(rows_in, full_up, preferred_element_type=jnp.float32)
    grad_hidden = contract_last(cot_in, complete_down_weight)
    sigmoid_gate = jax.nn.sigmoid(pre_gate)
    activated = pre_gate * sigmoid_gate
    hidden = (activated * pre_up).astype(jnp.bfloat16)
    grad_gate_pre = (
        grad_hidden * pre_up * sigmoid_gate * (1.0 + pre_gate * (1.0 - sigmoid_gate))
    ).astype(jnp.bfloat16)
    grad_up_pre = (grad_hidden * activated).astype(jnp.bfloat16)
    joint_grad = jnp.concatenate([grad_gate_pre, grad_up_pre], axis=1)
    columns = rows_in
    summed = lax.psum_scatter(
        contract_first(columns, joint_grad).astype(jnp.bfloat16),
        "tensor",
        scatter_dimension=0,
        tiled=True,
    ).astype(jnp.float32)
    columns = hidden
    summed_down = lax.psum_scatter(
        contract_first(columns, cot_in).astype(jnp.bfloat16),
        "tensor",
        scatter_dimension=0,
        tiled=True,
    )
    rows_out = (
        contract_last(grad_gate_pre, full_gate) + contract_last(grad_up_pre, full_up)
    ).astype(jnp.bfloat16)
    returned = lax.all_to_all(
        rows_out.reshape(experts, capacity, model_width),
        "expert",
        split_axis=0,
        concat_axis=0,
        tiled=True,
    )
    returned = returned.reshape(slots_all, model_width)
    gathered = returned[jnp.minimum(target, slots_all - 1)].astype(jnp.float32)
    gathered = jnp.where(retained[:, None], gathered, jnp.zeros((), jnp.float32))
    input_grad = jnp.sum(gathered.reshape(tok_rows, 2, model_width), axis=1).astype(jnp.bfloat16)
    return (
        input_grad,
        summed[:, :hidden_width].astype(jnp.bfloat16)[None],
        summed[:, hidden_width:].astype(jnp.bfloat16)[None],
        summed_down[None],
    )


def solution(mesh):
    return jax.shard_map(
        local,
        mesh=mesh,
        in_specs=(
            P(("group", "expert", "tensor"), None),
            P(("group", "expert", "tensor"), None),
            P(("group", "expert", "tensor"), None),
            P(("group", "expert", "tensor"), None),
            P("expert", "tensor", None),
            P("expert", "tensor", None),
            P("expert", "tensor", None),
        ),
        out_specs=(
            P(("group", "expert", "tensor"), None),
            P(("group", "expert"), "tensor", None),
            P(("group", "expert"), "tensor", None),
            P(("group", "expert"), "tensor", None),
        ),
        check_vma=False,
    )
```

profile of v0, /device:TPU:33, one launch (start us, length us, event | category | flops | bytes accessed | tf_op | source)
XLA Modules:
  0.0 268.5 jit_solution(17114819456044467848)
XLA Ops:
  11.3 2.2 gather_fusion.1
  13.5 1.8 reshape.120
  15.5 1.2 gather_fusion
  17.0 2.2 gather_fusion.2
  19.2 2.2 gather.17
  21.4 3.6 %fusion.10 = (bf16[32,4,4096]{2,1,0:T(4,128)(2,1)}, bf16[32,4,4096]{2,1,0:T(4,128)(2,1)}) fusion(f32[32,4,4096]{2,1,0:T(4,128)S(1)} %reshape.120, f32[32,4]{1,0:T(8,128)S(1)} %mul.55, pred[32,4]{1,0:T(8,128)(4,1)S(1)} %broadcast_in_dim.63, bf16[32,4,4096]{2,1,0:T(4,128)(2,1)} %gather.17), kind=kLoop, calls=%fused_computation.20 | loop fusion | flops 2097152 | bytes 5243520 | tf_op jit(solution)/shard_map/jit(_where)/select_n | solution.py:41
  25.0 25.6 %all-to-all-start.1 = ((bf16[32,4,4096]{2,1,0:T(4,128)(2,1)}), bf16[32,4,4096]{2,1,0:T(4,128)(2,1)S(1)}, u32[]{:S(2)}, u32[]{:S(2)}) async-start(bf16[32,4,4096]{2,1,0:T(4,128)(2,1)} %get-tuple-element.9), calls=%async_computation.1 | async-start | bytes 2097152 | tf_op jit(solution)/shard_map/all_to_all | solution.py:43
  51.4 54.7 %all-to-all-done.1 = bf16[32,4,4096]{2,1,0:T(4,128)(2,1)S(1)} async-done(((bf16[32,4,4096]{2,1,0:T(4,128)(2,1)}), bf16[32,4,4096]{2,1,0:T(4,128)(2,1)S(1)}, u32[]{:S(2)}, u32[]{:S(2)}) %all-to-all-start.1) | async-done | bytes 1048608 | tf_op jit(solution)/shard_map/all_to_all | solution.py:43
  106.1 5.0 %all-to-all-start = ((bf16[32,4,4096]{2,1,0:T(4,128)(2,1)}), bf16[32,4,4096]{2,1,0:T(4,128)(2,1)}, u32[]{:S(2)}, u32[]{:S(2)}) async-start(bf16[32,4,4096]{2,1,0:T(4,128)(2,1)} %get-tuple-element.8), calls=%async_computation | async-start | bytes 2097152 | tf_op jit(solution)/shard_map/all_to_all | solution.py:50
  112.2 54.5 %all-to-all-done = bf16[32,4,4096]{2,1,0:T(4,128)(2,1)} async-done(((bf16[32,4,4096]{2,1,0:T(4,128)(2,1)}), bf16[32,4,4096]{2,1,0:T(4,128)(2,1)}, u32[]{:S(2)}, u32[]{:S(2)}) %all-to-all-start) | async-done | bytes 1048608 | tf_op jit(solution)/shard_map/all_to_all | solution.py:50
  166.8 1.3 reshape.116
  168.1 2.0 fusion.3
  170.2 2.0 fusion.6
  172.3 2.4 multiply_convert_fusion.2
  174.7 3.2 %convolution_convert_fusion = bf16[4096,512]{1,0:T(8,128)(2,1)} fusion(bf16[128,4096]{1,0:T(8,128)(2,1)S(1)} %reshape.117, bf16[128,256]{1,0:T(8,128)(2,1)S(1)} %get-tuple-element.6, bf16[128,256]{1,0:T(8,128)(2,1)S(1)} %get-tuple-element.7), kind=kOutput, calls=%fused_computation.5 | convolution fusion | flops 539230208 | bytes 5373952 | tf_op jit(solution)/shard_map/dot_general | solution.py:14
  178.0 2.5 fusion.1
  182.6 4.9 %all-to-all-start.2 = ((bf16[32,4,4096]{2,1,0:T(4,128)(2,1)}), bf16[32,4,4096]{2,1,0:T(4,128)(2,1)S(1)}, u32[]{:S(2)}, u32[]{:S(2)}) async-start(bf16[32,4,4096]{2,1,0:T(4,128)(2,1)} %reshape.118), calls=%async_computation.2 | async-start | bytes 2097152 | tf_op jit(solution)/shard_map/all_to_all | solution.py:97
  187.8 2.1 convolution_convert_fusion.1
  190.2 53.0 %all-to-all-done.2 = bf16[32,4,4096]{2,1,0:T(4,128)(2,1)S(1)} async-done(((bf16[32,4,4096]{2,1,0:T(4,128)(2,1)}), bf16[32,4,4096]{2,1,0:T(4,128)(2,1)S(1)}, u32[]{:S(2)}, u32[]{:S(2)}) %all-to-all-start.2) | async-done | bytes 1048608 | tf_op jit(solution)/shard_map/all_to_all | solution.py:97
  243.5 2.2 gather_fusion.3
  245.7 2.4 reshape.121
  248.0 4.8 %select_reduce_fusion = bf16[64,4096]{1,0:T(8,128)(2,1)} fusion(f32[64,2,4096]{2,1,0:T(2,128)S(1)} %reshape.121, pred[64,2]{1,0:T(8,128)(4,1)S(1)} %lt.48), kind=kLoop, calls=%fused_computation.18 | loop fusion | flops 786432 | bytes 2621568 | tf_op jit(solution)/shard_map/reduce_sum | solution.py:107
  252.9 2.3 slice_bitcast_fusion
  255.1 6.8 %reduce-scatter.5.cloned.1.call-done = bf16[64,4096]{1,0:T(8,128)(2,1)} async-done(((bf16[256,4096]{1,0:T(8,128)(2,1)}), bf16[64,4096]{1,0:T(8,128)(2,1)}) %reduce-scatter.5.cloned.1.call-update) | async-done | bytes 524304 | tf_op jit(solution)/shard_map/reduce_scatter | solution.py:88
  (47 shorter events, 9.3 us)
Async XLA Ops:
  7.2 4.1 %copy-start = (bf16[64,4096]{1,0:T(8,128)(2,1)S(1)}, bf16[64,4096]{1,0:T(8,128)(2,1)}, u32[]{:S(2)}) copy-start(bf16[64,4096]{1,0:T(8,128)(2,1)} %param.8) | copy-start | bytes 1572868
  7.2 160.9 %all-gather.11.cloned.1.call-start = ((), (), s32[]{:S(2)}) async-start(), calls=%async_computation.9 | async-start | bytes 2621440 | tf_op jit(solution)/shard_map/all_gather | solution.py:65
  13.5 1.8 copy-start.3
  13.5 3.5 %copy-start.1 = (bf16[64,4096]{1,0:T(8,128)(2,1)S(1)}, bf16[64,4096]{1,0:T(8,128)(2,1)}, u32[]{:S(2)}) copy-start(bf16[64,4096]{1,0:T(8,128)(2,1)} %param.7) | copy-start | bytes 1572868
  25.0 81.1 %all-to-all-start.1 = ((bf16[32,4,4096]{2,1,0:T(4,128)(2,1)}), bf16[32,4,4096]{2,1,0:T(4,128)(2,1)S(1)}, u32[]{:S(2)}, u32[]{:S(2)}) async-start(bf16[32,4,4096]{2,1,0:T(4,128)(2,1)} %get-tuple-element.9), calls=%async_computation.1 | async-start | bytes 2097152 | tf_op jit(solution)/shard_map/all_to_all | solution.py:43
  50.6 119.6 %all-gather.9.cloned.1.call-start = ((), (), s32[]{:S(2)}) async-start(), calls=%async_computation.8 | async-start | bytes 2621440 | tf_op jit(solution)/shard_map/all_gather | solution.py:66
  106.1 60.7 %all-to-all-start = ((bf16[32,4,4096]{2,1,0:T(4,128)(2,1)}), bf16[32,4,4096]{2,1,0:T(4,128)(2,1)}, u32[]{:S(2)}, u32[]{:S(2)}) async-start(bf16[32,4,4096]{2,1,0:T(4,128)(2,1)} %get-tuple-element.8), calls=%async_computation | async-start | bytes 2097152 | tf_op jit(solution)/shard_map/all_to_all | solution.py:50
  111.1 61.2 %all-gather.7.cloned.1.call-start = ((), (), s32[]{:S(2)}) async-start(), calls=%async_computation.7 | async-start | bytes 2621440 | tf_op jit(solution)/shard_map/all_gather | solution.py:67
  111.9 141.0 %reduce-scatter.3.cloned.1.call-start = ((), (), s32[]{:S(2)}) async-start(), calls=%async_computation.5 | async-start | bytes 5242880 | tf_op jit(solution)/shard_map/reduce_scatter | solution.py:81
  178.0 2.6 copy-start.2
  182.6 60.6 %all-to-all-start.2 = ((bf16[32,4,4096]{2,1,0:T(4,128)(2,1)}), bf16[32,4,4096]{2,1,0:T(4,128)(2,1)S(1)}, u32[]{:S(2)}, u32[]{:S(2)}) async-start(bf16[32,4,4096]{2,1,0:T(4,128)(2,1)} %reshape.118), calls=%async_computation.2 | async-start | bytes 2097152 | tf_op jit(solution)/shard_map/all_to_all | solution.py:97
  187.6 74.3 %reduce-scatter.5.cloned.1.call-start = ((), (), s32[]{:S(2)}) async-start(), calls=%async_computation.6 | async-start | bytes 2621440 | tf_op jit(solution)/shard_map/reduce_scatter | solution.py:88
Sparse Core Ops, SparseCore 0:
  9.8 51.2 all-gather.10
  63.0 36.8 all-gather.8
  113.7 38.3 all-gather.6
  178.1 45.2 reduce-scatter.2
  226.4 35.5 reduce-scatter.4
where the time goes:
time: 269 us; the launch traced here: 268 us
  waiting for transfers between devices  171 us (64%)
  starting transfers between devices  36 us (13%)
  local copies, waits for them, and re-layouts  22.3 us (8%)
  matrix products  15.2 us (6%)
  between operations  14.1 us (5%)
  other arithmetic  9.57 us (4%)
    all_to_all x1, waiting for transfers between devices, local(): lax.all_to_all(send_rows.reshape(experts, capacity, model_width), 'expert...  54.7 us
    all_to_all x1, waiting for transfers between devices, local(): lax.all_to_all(send_cot.reshape(experts, capacity, model_width), 'expert'...  54.5 us
    all_to_all x1, waiting for transfers between devices, local(): lax.all_to_all(rows_out.reshape(experts, capacity, model_width), 'expert'...  53 us
    all_to_all x1, starting transfers between devices, local(): lax.all_to_all(send_rows.reshape(experts, capacity, model_width), 'expert...  25.6 us
    reduce_scatter x1, waiting for transfers between devices, local(): lax.psum_scatter(contract_first(columns, cot_in).astype(jnp.bfloat16), 't...  6.78 us
    dot_general x3, matrix products, contract_last(): lax.dot_general(left, right, (((1,), (1,)), ((), ())), preferred_element_...  5.8 us
  transfers between devices with their start and end apart: 8, of which 4 were waited for; matrix products, arithmetic and copies ran while one was open for 15% of the time, Pallas kernels for 0%

commit v1 on v0

v1 whole, which is shorter than its diff:
```python
import functools

import jax
import jax.numpy as jnp
from jax import lax
from jax.experimental import pallas as pl
from jax.experimental.pallas import tpu as pltpu
from jax.sharding import PartitionSpec as P

BF = jnp.bfloat16
F32 = jnp.float32
MESH = pl.DeviceIdType.MESH


def dot(a, b, ca=1, cb=0):
    return lax.dot_general(a, b, (((ca,), (cb,)), ((), ())), preferred_element_type=F32)


def iota(shape, axis):
    return lax.broadcasted_iota(jnp.int32, shape, axis)


def body(
    sizes,
    ids_ref, gts_ref, tok_hbm, cot_hbm, wg_hbm, wu_hbm, wd_hbm,
    ig_ref, gg_ref, gu_ref, gd_ref,
    tokv, cotv, wg, wu, wd, pick, send, recv, rq, cq, gact, hid, rsend, ret,
    xrow, xact, down, xdown,
    in_sem, ssem, rsem, wssem, wrsem, bssem, brsem, rowss, rowrs, actss, actrs, dss, drs,
):
    E, T, CAP, TOK, D, FF = sizes
    Z = E // 2
    DT = D // T
    FT = FF // T
    ROWS = T * CAP
    GRP = 8
    NG = E // GRP
    GS = GRP * CAP
    SL = E * CAP
    me = lax.axis_index("expert")
    ti = lax.axis_index("tensor")

    def partner(j, sign):
        u = j // 2
        near = (u + 1) // 2
        step = (u % 2) * near + (1 - u % 2) * (Z - near)
        away = step if sign > 0 else Z - step
        return ((me // 2 + away) % Z) * 2 + (me % 2 + j) % 2

    def side(k):
        return (ti + k) % T

    loads = []

    def load(src, dst, k):
        c = pltpu.make_async_copy(src, dst, in_sem.at[k])
        c.start()
        return c

    for q in range(T):
        loads.append(load(tok_hbm.at[:, pl.ds(q * DT, DT)], tokv.at[pl.ds(q * TOK, TOK)], q))
    for q in range(T):
        loads.append(load(cot_hbm.at[:, pl.ds(q * DT, DT)], cotv.at[pl.ds(q * TOK, TOK)], T + q))
    loads.append(load(wg_hbm.at[0], wg.at[ti], 2 * T))
    loads.append(load(wu_hbm.at[0], wu.at[ti], 2 * T + 1))
    loads.append(load(wd_hbm.at[0], wd.at[ti], 2 * T + 2))

    bar = pltpu.get_barrier_semaphore()

    def greet(j, c):
        pl.semaphore_signal(bar, 1, device_id={"expert": partner(j, 1)}, device_id_type=MESH)
        return c

    lax.fori_loop(1, E, greet, 0)
    for k in range(1, T):
        pl.semaphore_signal(bar, 1, device_id={"tensor": side(k)}, device_id_type=MESH)

    W = T * TOK
    i0 = ids_ref[0:1, :]
    i1 = ids_ref[1:2, :]
    ex = iota((E, W), 0)
    h0 = i0 == ex
    h1 = i1 == ex
    both = (jnp.where(h0, 1.0, 0.0) + jnp.where(h1, 1.0, 0.0)).astype(BF)
    ra = iota((W, W), 0)
    rb = iota((W, W), 1)
    before = jnp.where((ra // TOK == rb // TOK) & (ra < rb), 1.0, 0.0).astype(BF)
    count = dot(both, before)
    p0 = jnp.sum(jnp.where(h0, count, 0.0), axis=0, keepdims=True).astype(jnp.int32)
    p1 = jnp.sum(jnp.where(h1, count, 0.0), axis=0, keepdims=True).astype(jnp.int32)
    s0 = jnp.where(p0 < CAP, i0 * CAP + p0, -1)
    s1 = jnp.where(p1 < CAP, i1 * CAP + p1, -1)
    g0 = gts_ref[0:1, :]
    g1 = gts_ref[1:2, :]

    for c in loads[: 2 * T]:
        c.wait()

    EB = 4
    RB = EB * ROWS

    def build(i, c):
        r = iota((RB, W), 0) + i * RB
        slot = (r // ROWS) * CAP + r % CAP
        same = (r // CAP) % T == iota((RB, W), 1) // TOK
        m0 = (s0 == slot) & same
        m1 = (s1 == slot) & same
        o = jnp.where(m0 | m1, 1.0, 0.0).astype(BF)
        gate = jnp.sum(jnp.where(m0, g0, 0.0) + jnp.where(m1, g1, 0.0), axis=1, keepdims=True)
        pick[pl.ds(i * RB, RB), :] = o
        x = dot(o, tokv[...]).astype(BF)
        send[pl.ds(i * EB, EB), 0:ROWS, :] = x.reshape(EB, ROWS, DT)
        y = (gate * dot(o, cotv[...])).astype(BF)
        send[pl.ds(i * EB, EB), ROWS : 2 * ROWS, :] = y.reshape(EB, ROWS, DT)
        return c

    lax.fori_loop(0, E // EB, build, 0)

    pl.semaphore_wait(bar, E - 1 + T - 1)

    def dispatch(j):
        to = partner(j, 1)
        return pltpu.make_async_remote_copy(
            send.at[to], recv.at[j], ssem.at[j], rsem.at[j],
            device_id={"expert": to}, device_id_type=MESH,
        )

    def start_dispatch(j, c):
        dispatch(j).start()
        return c

    lax.fori_loop(1, E, start_dispatch, 0)

    weights = (wg, wu, wd)

    def gather(n, k):
        return pltpu.make_async_remote_copy(
            weights[n].at[ti], weights[n].at[ti], wssem.at[n, k], wrsem.at[n, k],
            device_id={"tensor": side(k)}, device_id_type=MESH,
        )

    def gathered(n, k):
        src = side(T - k)
        return pltpu.make_async_remote_copy(
            weights[n].at[src], weights[n].at[src], wssem.at[n, k], wrsem.at[n, k],
            device_id={"tensor": side(k)}, device_id_type=MESH,
        )

    for n in range(3):
        loads[2 * T + n].wait()
    for n in range(3):
        for k in (1, 3, 2):
            gather(n, k).start()

    recv[0] = send[me]

    MB = 2 * ROWS
    fo = iota((GRP * MB, GRP * MB), 0)
    fi = iota((GRP * MB, GRP * MB), 1)
    want = (((fo % GS) // CAP) * MB) + (fo // (T * GS)) * ROWS + ((fo // GS) % T) * CAP + fo % CAP
    spread = jnp.where(fi == want, 1.0, 0.0).astype(BF)
    bo = iota((GRP * ROWS, GRP * ROWS), 0)
    bi = iota((GRP * ROWS, GRP * ROWS), 1)
    wantb = ((bo // CAP) % T) * GS + (bo // ROWS) * CAP + bo % CAP
    fold = jnp.where(bi == wantb, 1.0, 0.0).astype(BF)

    def wait_dispatch(j, c):
        dispatch(j).wait_recv()
        return c

    def unpack(g):
        lax.fori_loop(max(1, g * GRP), (g + 1) * GRP, wait_dispatch, 0)
        for half in range(2):
            cols = pl.ds(half * (DT // 2), DT // 2)
            m = recv[pl.ds(g * GRP, GRP), :, cols].reshape(GRP * MB, DT // 2)
            v = dot(spread, m).astype(BF)
            for q in range(T):
                rq[q, pl.ds(g * GS, GS), cols] = v[q * GS : (q + 1) * GS]
                cq[q, pl.ds(g * GS, GS), cols] = v[(T + q) * GS : (T + q + 1) * GS]

    def back(j):
        to = partner(j, -1)
        return pltpu.make_async_remote_copy(
            rsend.at[j], ret.at[me], bssem.at[j], brsem.at[me],
            device_id={"expert": to}, device_id_type=MESH,
        )

    def start_back(j, c):
        back(j).start()
        return c

    def expert(lo, hi):
        sl = pl.ds(lo * GS, (hi - lo) * GS)
        pg = sum(dot(rq[q, sl, :], wg[q]) for q in range(T))
        pu = sum(dot(rq[q, sl, :], wu[q]) for q in range(T))
        gh = sum(
            dot(cq[q, sl, :], wd[:, :, q * DT : (q + 1) * DT].reshape(FF, DT), 1, 1)
            for q in range(T)
        )
        sg = jax.nn.sigmoid(pg)
        act = pg * sg
        hid[sl, :] = (act * pu).astype(BF)
        a = (gh * pu * sg * (1.0 + pg * (1.0 - sg))).astype(BF)
        b = (gh * act).astype(BF)
        gact[sl, 0:FF] = a
        gact[sl, FF : 2 * FF] = b
        parts = [(dot(a, wg[q], 1, 1) + dot(b, wu[q], 1, 1)).astype(BF) for q in range(T)]
        for g in range(lo, hi):
            o = (g - lo) * GS
            m = jnp.concatenate([p[o : o + GS] for p in parts], axis=0)
            v = dot(fold, m).astype(BF)
            rsend[pl.ds(g * GRP, GRP)] = v.reshape(GRP, ROWS, DT)
        lax.fori_loop(max(1, lo * GRP), hi * GRP, start_back, 0)

    def rows_to(h, k):
        lo, n = (0, (NG - 1) * GS) if h == 0 else ((NG - 1) * GS, GS)
        return pltpu.make_async_remote_copy(
            rq.at[side(k), pl.ds(lo, n)], xrow.at[ti, pl.ds(lo, n)], rowss.at[h, k], rowrs.at[h, k],
            device_id={"tensor": side(k)}, device_id_type=MESH,
        )

    def act_to(k):
        return pltpu.make_async_remote_copy(
            gact, xact.at[ti], actss.at[k], actrs.at[k],
            device_id={"tensor": side(k)}, device_id_type=MESH,
        )

    def down_to(k):
        return pltpu.make_async_remote_copy(
            down.at[side(k)], xdown.at[ti], dss.at[k], drs.at[k],
            device_id={"tensor": side(k)}, device_id_type=MESH,
        )

    for g in range(NG - 1):
        unpack(g)
    for k in (1, 3, 2):
        rows_to(0, k).start()
    for n in range(3):
        for k in range(1, T):
            gathered(n, k).wait_recv()
    expert(0, NG - 1)
    unpack(NG - 1)
    expert(NG - 1, NG)
    for k in (1, 3, 2):
        rows_to(1, k).start()
        act_to(k).start()

    ht = hid[...].astype(F32).T.astype(BF)
    for q in range(T):
        v = dot(ht, cq[q]).astype(BF)
        for t in range(T):
            down[t, :, q * DT : (q + 1) * DT] = v[t * FT : (t + 1) * FT]
    for k in (1, 3, 2):
        down_to(k).start()

    xrow[ti] = rq[ti]
    xact[ti] = gact[...]
    ret[me] = rsend[0]
    xdown[ti] = down[ti]
    for k in range(1, T):
        rows_to(0, k).wait_recv()
        rows_to(1, k).wait_recv()
        act_to(k).wait_recv()
    acts = xact[...].reshape(T * SL, 2 * FF)
    CB = 256
    for n in range(DT // CB):
        r = xrow[:, :, n * CB : (n + 1) * CB].reshape(T * SL, CB)
        v = dot(r, acts, 0, 0).astype(BF)
        gg_ref[0, n * CB : (n + 1) * CB, :] = v[:, 0:FF]
        gu_ref[0, n * CB : (n + 1) * CB, :] = v[:, FF : 2 * FF]

    for k in range(1, T):
        down_to(k).wait_recv()
    for n in range(T):
        cols = pl.ds(n * DT, DT)
        v = xdown[0, :, cols].astype(F32)
        for t in range(1, T):
            v = v + xdown[t, :, cols].astype(F32)
        gd_ref[0, :, cols] = v.astype(BF)

    unpick = pick[...].astype(F32).T.astype(BF)

    def wait_back(j, c):
        src = partner(j, 1)
        pltpu.make_async_remote_copy(
            rsend.at[j], ret.at[src], bssem.at[j], brsem.at[src],
            device_id={"expert": src}, device_id_type=MESH,
        ).wait_recv()
        return c

    lax.fori_loop(1, E, wait_back, 0)
    for n in range(DT // CB):
        r = ret[:, :, n * CB : (n + 1) * CB].reshape(E * ROWS, CB)
        v = dot(unpick, r).astype(BF)
        for q in range(T):
            ig_ref[:, q * DT + n * CB : q * DT + (n + 1) * CB] = v[q * TOK : (q + 1) * TOK]

    def drain(j, c):
        dispatch(j).wait_send()
        back(j).wait_send()
        return c

    lax.fori_loop(1, E, drain, 0)
    for k in range(1, T):
        for n in range(3):
            gather(n, k).wait_send()
        rows_to(0, k).wait_send()
        rows_to(1, k).wait_send()
        act_to(k).wait_send()
        down_to(k).wait_send()


def local(tokens, cotangent, expert_ids, gate_wts, w_gate, w_up, w_down):
    TOK, D = tokens.shape
    E = lax.axis_size("expert")
    T = lax.axis_size("tensor")
    FF = w_gate.shape[2]
    CAP = 2 * TOK // E
    DT, FT, SL, ROWS = D // T, FF // T, E * CAP, T * CAP
    ids = jnp.tile(expert_ids.T, (1, T))
    gts = jnp.tile(gate_wts.T, (1, T))
    vm = pl.BlockSpec(memory_space=pltpu.VMEM)
    hb = pl.BlockSpec(memory_space=pl.ANY)
    dma = pltpu.SemaphoreType.DMA
    return pl.pallas_call(
        functools.partial(body, (E, T, CAP, TOK, D, FF)),
        name="routed_backward",
        out_shape=(
            jax.ShapeDtypeStruct((TOK, D), BF),
            jax.ShapeDtypeStruct((1, DT, FF), BF),
            jax.ShapeDtypeStruct((1, DT, FF), BF),
            jax.ShapeDtypeStruct((1, FT, D), BF),
        ),
        in_specs=[vm, vm, hb, hb, hb, hb, hb],
        out_specs=(vm, vm, vm, vm),
        scratch_shapes=[
            pltpu.VMEM((T * TOK, DT), BF),
            pltpu.VMEM((T * TOK, DT), BF),
            pltpu.VMEM((T, DT, FF), BF),
            pltpu.VMEM((T, DT, FF), BF),
            pltpu.VMEM((T, FT, D), BF),
            pltpu.VMEM((E * ROWS, T * TOK), BF),
            pltpu.VMEM((E, 2 * ROWS, DT), BF),
            pltpu.VMEM((E, 2 * ROWS, DT), BF),
            pltpu.VMEM((T, SL, DT), BF),
            pltpu.VMEM((T, SL, DT), BF),
            pltpu.VMEM((SL, 2 * FF), BF),
            pltpu.VMEM((SL, FF), BF),
            pltpu.VMEM((E, ROWS, DT), BF),
            pltpu.VMEM((E, ROWS, DT), BF),
            pltpu.VMEM((T, SL, DT), BF),
            pltpu.VMEM((T, SL, 2 * FF), BF),
            pltpu.VMEM((T, FT, D), BF),
            pltpu.VMEM((T, FT, D), BF),
            dma((2 * T + 3,)),
            dma((E,)), dma((E,)),
            dma((3, T)), dma((3, T)),
            dma((E,)), dma((E,)),
            dma((2, T)), dma((2, T)),
            dma((T,)), dma((T,)),
            dma((T,)), dma((T,)),
        ],
        compiler_params=pltpu.CompilerParams(
            collective_id=0, has_side_effects=True, vmem_limit_bytes=56 << 20
        ),
    )(ids, gts, tokens, cotangent, w_gate, w_up, w_down)


def solution(mesh):
    rows = P(("group", "expert", "tensor"), None)
    grads = P(("group", "expert"), "tensor", None)
    return jax.shard_map(
        local,
        mesh=mesh,
        in_specs=(rows, rows, rows, rows) + (P("expert", "tensor", None),) * 3,
        out_specs=(rows, grads, grads, grads),
        check_vma=False,
    )
```

time: 269 us -> 180 us (0.67)
  Pallas kernels: 0 us -> 172 us
  waiting for transfers between devices: 171 us -> 0 us
  starting transfers between devices: 36 us -> 0 us
  matrix products: 15.2 us -> 0 us
  local copies, waits for them, and re-layouts: 22.3 us -> 7.2 us
  between operations: 14.1 us -> 0.66 us
  other arithmetic: 9.57 us -> 0 us
    pallas_call x0 -> x1, Pallas kernels: none -> 172 us  [local(): pl.pallas_call(functools.partial(body, (E, T, CAP, TOK, D, FF)), name='ro...]
    all_to_all x3 -> x0, waiting for transfers between devices: 162 us -> none  [the longest x1 54.7 us: local(): lax.all_to_all(send_rows.reshape(experts, capacity, model_width), 'expert...]
    all_to_all x3 -> x0, starting transfers between devices: 35.5 us -> none  [the longest x1 25.6 us: local(): lax.all_to_all(send_rows.reshape(experts, capacity, model_width), 'expert...]
    dot_general x7 -> x0, matrix products: 15.2 us -> none  [the longest x3 5.8 us: contract_last(): lax.dot_general(left, right, (((1,), (1,)), ((), ())), preferred_element_...]
    gather x5 -> x0, local copies, waits for them, and re-layouts: 10 us -> none  [the longest x2 4.42 us: local(): send_rows = jnp.where(populated_rows[:, None], tokens[tok_index], zero_half)]
    reduce_scatter x2 -> x0, waiting for transfers between devices: 6.79 us -> none  [the longest x1 6.78 us: local(): lax.psum_scatter(contract_first(columns, cot_in).astype(jnp.bfloat16), 't...]
    reduce_sum x2 -> x0, other arithmetic: 5 us -> none  [the longest x1 4.83 us: local(): jnp.sum(gathered.reshape(tok_rows, 2, model_width), axis=1)]
    unnamed x10 -> x14, local copies, waits for them, and re-layouts: 0.88 us -> 5.87 us
  transfers between devices with their start and end apart: 8 -> 0, of which waited for: 4 -> 0; matrix products, arithmetic and copies ran while one was open for 15% -> 0% of each run, Pallas kernels for 0% -> 0%
where the time goes in v1:
time: 180 us
  Pallas kernels  172 us (96%)
  local copies, waits for them, and re-layouts  7.2 us (4%)
    pallas_call x1, Pallas kernels, local(): pl.pallas_call(functools.partial(body, (E, T, CAP, TOK, D, FF)), name='ro...  172 us
    unnamed x14, local copies, waits for them, and re-layouts  5.87 us

profile of v1, /device:TPU:33, one launch (start us, length us, event | category | flops | bytes accessed | tf_op | source)
XLA Modules:
  0.0 179.8 jit_solution(7742740862101124264)
XLA Ops:
  0.6 0.0 copy-start.3
  0.6 0.7 copy-done.3
  1.3 0.0 copy-start.4
  1.3 0.7 tile.9.ids_ref
  2.0 0.0 copy-done.4
  2.0 0.7 tile.21.gts_ref
  2.7 171.9 %routed_backward.1 = (bf16[64,4096]{1,0:T(8,128)(2,1)}, bf16[1,1024,256]{2,1,0:T(8,128)(2,1)}, bf16[1,1024,256]{2,1,0:T(8,128)(2,1)}, bf16[1,64,4096]{2,1,0:T(8,128)(2,1)}) custom-call(s32[2,256]{1,0:T(2,128)} %tile.9.ids_ref, f32[2,256]{1,0:T(2,128)} %tile.21.gts_ref, bf16[64,4096]{1,0:T(8,128)(2,1)} %tok_hbm.1, bf16[64,4096]{1,0:T(8,128)(2,1)} %cot_hbm.1, ...), custom_call_target="tpu_custom_call" | custom-call | tf_op jit(solution)/shard_map/routed_backward/pallas_call | solution.py:325
  174.6 0.0 copy-start.2
  174.6 1.9 %copy.15 = bf16[64,4096]{1,0:T(8,128)(2,1)} copy(bf16[64,4096]{1,0:T(8,128)(2,1)} %get-tuple-element.8) | data formatting | bytes 1048576
  176.5 0.0 copy-done.2
  176.5 0.0 copy-start.1
  176.5 0.8 copy.16
  177.3 0.4 copy-done.1
  177.8 0.0 copy-start
  177.8 0.8 copy.17
  178.6 0.4 copy-done
  179.0 0.8 copy.18
  (2 shorter events, 0.0 us)
Async XLA Ops:
  0.6 0.7 copy-start.3
  1.3 0.7 copy-start.4
  174.6 1.9 %copy-start.2 = (bf16[1,1024,256]{2,1,0:T(8,128)(2,1)S(1)}, bf16[1,1024,256]{2,1,0:T(8,128)(2,1)}, u32[]{:S(2)}) copy-start(bf16[1,1024,256]{2,1,0:T(8,128)(2,1)} %get-tuple-element.9) | copy-start | bytes 1572868
  176.5 1.2 copy-start.1
  177.8 1.2 copy-start

commit v2 on v1

v2 whole, which is shorter than its diff:
```python
import functools

import jax
import jax.numpy as jnp
from jax import lax
from jax.experimental import pallas as pl
from jax.experimental.pallas import tpu as pltpu
from jax.sharding import PartitionSpec as P

BF = jnp.bfloat16
F32 = jnp.float32
MESH = pl.DeviceIdType.MESH


def dot(a, b, ca=1, cb=0):
    return lax.dot_general(a, b, (((ca,), (cb,)), ((), ())), preferred_element_type=F32)


def iota(shape, axis):
    return lax.broadcasted_iota(jnp.int32, shape, axis)


def body(
    sizes,
    ids_hbm, gts_hbm, tok_hbm, cot_hbm, wg_hbm, wu_hbm, wd_hbm,
    ig_ref, gg_ref, gu_ref, gd_ref,
    idv, gtv, tokv, cotv, wg, wu, wd, pick, send, recv, rc, gact, rsend, ret, xrc, xact, down,
    from_up, from_below, in_sem, ssem, rsem, wssem, wrsem, bssem, brsem, rcss, rcrs, actss, actrs, dss, drs,
):
    E, T, CAP, TOK, D, FF = sizes
    Z = E // 2
    DT = D // T
    FT = FF // T
    ROWS = T * CAP
    GRP = 8
    NG = E // GRP
    GS = GRP * CAP
    SL = E * CAP
    me = lax.axis_index("expert")
    ti = lax.axis_index("tensor")

    def partner(j, sign):
        u = j // 2
        near = (u + 1) // 2
        step = (u % 2) * near + (1 - u % 2) * (Z - near)
        away = step if sign > 0 else Z - step
        return ((me // 2 + away) % Z) * 2 + (me % 2 + j) % 2

    def side(k):
        return (ti + k) % T

    bar = pltpu.get_barrier_semaphore()
    z, core = me // 2, me % 2
    up, below = (z + 1) % Z, (z + Z - 1) % Z
    near_by = [z * 2 + 1 - core, up * 2 + core, up * 2 + 1 - core, below * 2 + core, below * 2 + 1 - core]
    for e in near_by:
        pl.semaphore_signal(bar, 1, device_id={"expert": e}, device_id_type=MESH)
    for k in range(1, T):
        pl.semaphore_signal(bar, 1, device_id={"tensor": side(k)}, device_id_type=MESH)

    def tell_up(k):
        pl.semaphore_signal(from_below.at[k], 1, device_id={"expert": up * 2 + core}, device_id_type=MESH)

    def tell_below(k):
        pl.semaphore_signal(from_up.at[k], 1, device_id={"expert": below * 2 + core}, device_id_type=MESH)

    loads = []

    def load(src, dst, k):
        c = pltpu.make_async_copy(src, dst, in_sem.at[k])
        c.start()
        return c

    head = [load(ids_hbm, idv, 2 * T + 3), load(gts_hbm, gtv, 2 * T + 4)]
    for q in range(T):
        loads.append(load(tok_hbm.at[:, pl.ds(q * DT, DT)], tokv.at[pl.ds(q * TOK, TOK)], q))
    for q in range(T):
        loads.append(load(cot_hbm.at[:, pl.ds(q * DT, DT)], cotv.at[pl.ds(q * TOK, TOK)], T + q))
    loads.append(load(wg_hbm.at[0], wg.at[ti], 2 * T))
    loads.append(load(wu_hbm.at[0], wu.at[ti], 2 * T + 1))
    loads.append(load(wd_hbm.at[0], wd.at[ti], 2 * T + 2))

    W = T * TOK
    for c in head:
        c.wait()
    ids = jnp.concatenate([idv[...]] * T, axis=1)
    gts = jnp.concatenate([gtv[...]] * T, axis=1)
    i0 = ids[0:1, :]
    i1 = ids[1:2, :]
    ex = iota((E, W), 0)
    h0 = i0 == ex
    h1 = i1 == ex
    both = (jnp.where(h0, 1.0, 0.0) + jnp.where(h1, 1.0, 0.0)).astype(BF)
    ra = iota((W, W), 0)
    rb = iota((W, W), 1)
    before = jnp.where((ra // TOK == rb // TOK) & (ra < rb), 1.0, 0.0).astype(BF)
    count = dot(both, before)
    p0 = jnp.sum(jnp.where(h0, count, 0.0), axis=0, keepdims=True).astype(jnp.int32)
    p1 = jnp.sum(jnp.where(h1, count, 0.0), axis=0, keepdims=True).astype(jnp.int32)
    s0 = jnp.where(p0 < CAP, i0 * CAP + p0, -1)
    s1 = jnp.where(p1 < CAP, i1 * CAP + p1, -1)
    g0 = gts[0:1, :]
    g1 = gts[1:2, :]

    for c in loads[: 2 * T]:
        c.wait()

    EB = 4
    RB = EB * ROWS

    def dispatch(j):
        return pltpu.make_async_remote_copy(
            send.at[j], recv.at[j], ssem.at[j], rsem.at[j],
            device_id={"expert": partner(j, 1)}, device_id_type=MESH,
        )

    def build(i):
        r = iota((RB, 1), 0) + i * RB
        j = r // ROWS
        u = j // 2
        near = (u + 1) // 2
        step = jnp.where(u % 2 == 1, near, Z - near)
        slot = (((z + step) % Z) * 2 + (core + j) % 2) * CAP + r % CAP
        same = (r // CAP) % T == iota((1, W), 1) // TOK
        m0 = (s0 == slot) & same
        m1 = (s1 == slot) & same
        o = jnp.where(m0 | m1, 1.0, 0.0).astype(BF)
        gate = jnp.sum(jnp.where(m0, g0, 0.0) + jnp.where(m1, g1, 0.0), axis=1, keepdims=True)
        pick[pl.ds(i * RB, RB), :] = o
        x = dot(o, tokv[...]).astype(BF)
        send[pl.ds(i * EB, EB), 0:ROWS, :] = x.reshape(EB, ROWS, DT)
        y = (gate * dot(o, cotv[...])).astype(BF)
        send[pl.ds(i * EB, EB), ROWS : 2 * ROWS, :] = y.reshape(EB, ROWS, DT)

    weights = (wg, wu, wd)

    def gather(n, k):
        return pltpu.make_async_remote_copy(
            weights[n].at[ti], weights[n].at[ti], wssem.at[n, k], wrsem.at[n, k],
            device_id={"tensor": side(1 if k == 0 else T - 1)}, device_id_type=MESH,
        )

    def gathered(n, k):
        src = side(T - 1 if k == 0 else 1)
        return pltpu.make_async_remote_copy(
            weights[n].at[src], weights[n].at[src], wssem.at[n, k], wrsem.at[n, k],
            device_id={"tensor": side(1)}, device_id_type=MESH,
        )

    def pass_on(n, k):
        h = weights[n].shape[1] // 2
        part = weights[n].at[side(T - 1 if k == 0 else 1), pl.ds(k * h, h)]
        return pltpu.make_async_remote_copy(
            part, part, wssem.at[n, 2 + k], wrsem.at[n, 2 + k],
            device_id={"tensor": side(1 if k == 0 else T - 1)}, device_id_type=MESH,
        )

    def passed_on(n, k):
        h = weights[n].shape[1] // 2
        part = weights[n].at[side(2), pl.ds(k * h, h)]
        return pltpu.make_async_remote_copy(
            part, part, wssem.at[n, 2 + k], wrsem.at[n, 2 + k],
            device_id={"tensor": side(1)}, device_id_type=MESH,
        )

    build(0)
    pl.semaphore_wait(bar, len(near_by) + T - 1)
    tell_below(1)
    tell_up(1)
    for j in range(1, EB):
        dispatch(j).start()
    for n in range(3):
        loads[2 * T + n].wait()
    for n in range(3):
        for k in range(2):
            gather(n, k).start()
    NC = E // EB

    def chunk(i, c):
        build(i)
        pl.semaphore_wait(from_up.at[i], 1)

        @pl.when(i < NC - 1)
        def _():
            tell_below(i + 1)

        @pl.when(i > 1)
        def _():
            pl.semaphore_wait(from_below.at[i - 1], 1)

            @pl.when(i < NC - 1)
            def _():
                tell_up(i)

        for j in range(EB):
            dispatch(i * EB + j).start()
        return c

    lax.fori_loop(1, NC, chunk, 0)
    recv[0] = send[0]

    MB = 2 * ROWS
    fo = iota((GRP * MB, GRP * MB), 0)
    fi = iota((GRP * MB, GRP * MB), 1)
    want = (((fo % GS) // CAP) * MB) + (fo // (T * GS)) * ROWS + ((fo // GS) % T) * CAP + fo % CAP
    spread = jnp.where(fi == want, 1.0, 0.0).astype(BF)
    bo = iota((GRP * ROWS, GRP * ROWS), 0)
    bi = iota((GRP * ROWS, GRP * ROWS), 1)
    wantb = ((bo // CAP) % T) * GS + (bo // ROWS) * CAP + bo % CAP
    fold = jnp.where(bi == wantb, 1.0, 0.0).astype(BF)

    def wait_dispatch(j, c):
        dispatch(j).wait_recv()
        return c

    def unpack(g):
        lax.fori_loop(max(1, g * GRP), (g + 1) * GRP, wait_dispatch, 0)
        for half in range(2):
            cols = pl.ds(half * (DT // 2), DT // 2)
            m = recv[pl.ds(g * GRP, GRP), :, cols].reshape(GRP * MB, DT // 2)
            v = dot(spread, m).astype(BF)
            for q in range(T):
                rc[q, pl.ds(g * GS, GS), cols] = v[q * GS : (q + 1) * GS]
                cols2 = pl.ds(DT + half * (DT // 2), DT // 2)
                rc[q, pl.ds(g * GS, GS), cols2] = v[(T + q) * GS : (T + q + 1) * GS]

    def back(j):
        to = partner(j, -1)
        return pltpu.make_async_remote_copy(
            rsend.at[j], ret.at[j], bssem.at[j], brsem.at[j],
            device_id={"expert": to}, device_id_type=MESH,
        )

    def start_back(j, c):
        back(j).start()
        return c

    def expert(lo, hi):
        sl = pl.ds(lo * GS, (hi - lo) * GS)
        pg = sum(dot(rc[q, sl, 0:DT], wg[q]) for q in range(T))
        pu = sum(dot(rc[q, sl, 0:DT], wu[q]) for q in range(T))
        gh = sum(
            dot(rc[q, sl, DT : 2 * DT], wd[:, :, q * DT : (q + 1) * DT].reshape(FF, DT), 1, 1)
            for q in range(T)
        )
        sg = jax.nn.sigmoid(pg)
        act = pg * sg
        gact[sl, 2 * FF : 3 * FF] = (act * pu).astype(BF)
        a = (gh * pu * sg * (1.0 + pg * (1.0 - sg))).astype(BF)
        b = (gh * act).astype(BF)
        gact[sl, 0:FF] = a
        gact[sl, FF : 2 * FF] = b
        parts = [(dot(a, wg[q], 1, 1) + dot(b, wu[q], 1, 1)).astype(BF) for q in range(T)]
        for g in range(lo, hi):
            o = (g - lo) * GS
            m = jnp.concatenate([p[o : o + GS] for p in parts], axis=0)
            v = dot(fold, m).astype(BF)
            rsend[pl.ds(g * GRP, GRP)] = v.reshape(GRP, ROWS, DT)
        lax.fori_loop(max(1, lo * GRP), hi * GRP, start_back, 0)

    def part_of(h):
        return pl.ds(0, (NG - 1) * GS) if h == 0 else pl.ds((NG - 1) * GS, GS)

    def rows_to(h, k):
        return pltpu.make_async_remote_copy(
            rc.at[side(k), part_of(h)], xrc.at[ti, part_of(h)], rcss.at[h, k], rcrs.at[h, k],
            device_id={"tensor": side(k)}, device_id_type=MESH,
        )

    def act_to(h, k):
        return pltpu.make_async_remote_copy(
            gact.at[part_of(h)], xact.at[ti, part_of(h)], actss.at[h, k], actrs.at[h, k],
            device_id={"tensor": side(k)}, device_id_type=MESH,
        )

    mine = pl.ds(pl.multiple_of(ti * DT, DT), DT)

    def down_to(k):
        return pltpu.make_async_remote_copy(
            down.at[side(k)], gd_ref.at[0, :, mine], dss.at[k], drs.at[k],
            device_id={"tensor": side(k)}, device_id_type=MESH,
        )

    unpack(0)
    unpack(1)
    for n in range(3):
        for k in range(2):
            gathered(n, k).wait_recv()
            pass_on(n, k).start()
    for g in range(2, NG - 1):
        unpack(g)
    for k in (1, 3, 2):
        rows_to(0, k).start()
    for n in range(3):
        for k in range(2):
            passed_on(n, k).wait_recv()
    expert(0, NG - 1)
    for k in (1, 3, 2):
        act_to(0, k).start()
    unpack(NG - 1)
    for k in (1, 3, 2):
        rows_to(1, k).start()
    expert(NG - 1, NG)
    for k in (1, 3, 2):
        act_to(1, k).start()
    xrc[ti] = rc[ti]
    xact[ti] = gact[...]
    ret[0] = rsend[0]
    for h in range(2):
        for k in range(1, T):
            rows_to(h, k).wait_recv()
            act_to(h, k).wait_recv()
    CB = 256
    acts = xact[:, :, 2 * FF : 3 * FF].reshape(T * SL, FF)
    for n in range(DT // CB):
        r = xrc[:, :, DT + n * CB : DT + (n + 1) * CB].reshape(T * SL, CB)
        v = dot(acts, r, 0, 0).astype(BF)
        down[:, :, n * CB : (n + 1) * CB] = v.reshape(T, FT, CB)
    for k in (1, 3, 2):
        down_to(k).start()
    gd_ref[0, :, mine] = down[ti]
    acts = xact[:, :, 0 : 2 * FF].reshape(T * SL, 2 * FF)
    for n in range(DT // CB):
        r = xrc[:, :, n * CB : (n + 1) * CB].reshape(T * SL, CB)
        v = dot(r, acts, 0, 0).astype(BF)
        gg_ref[0, n * CB : (n + 1) * CB, :] = v[:, 0:FF]
        gu_ref[0, n * CB : (n + 1) * CB, :] = v[:, FF : 2 * FF]

    unpick = pick[...].astype(F32).T.astype(BF)

    def wait_back(j, c):
        back(j).wait_recv()
        return c

    lax.fori_loop(1, E, wait_back, 0)
    for n in range(DT // CB):
        r = ret[:, :, n * CB : (n + 1) * CB].reshape(E * ROWS, CB)
        v = dot(unpick, r).astype(BF)
        for q in range(T):
            ig_ref[:, q * DT + n * CB : q * DT + (n + 1) * CB] = v[q * TOK : (q + 1) * TOK]

    def drain(j, c):
        dispatch(j).wait_send()
        back(j).wait_send()
        return c

    lax.fori_loop(1, E, drain, 0)
    for n in range(3):
        for k in range(2):
            gather(n, k).wait_send()
            pass_on(n, k).wait_send()
    for k in range(1, T):
        for h in range(2):
            rows_to(h, k).wait_send()
            act_to(h, k).wait_send()
        down_to(k).wait_send()
        down_to(k).wait_recv()


def put(*refs):
    n = (len(refs) - 1) // 2
    copies = [pltpu.make_async_copy(refs[i], refs[n + i], refs[-1].at[i]) for i in range(n)]
    for c in copies:
        c.start()
    for c in copies:
        c.wait()


def local(tokens, cotangent, expert_ids, gate_wts, w_gate, w_up, w_down):
    TOK, D = tokens.shape
    E = lax.axis_size("expert")
    T = lax.axis_size("tensor")
    FF = w_gate.shape[2]
    CAP = 2 * TOK // E
    DT, FT, SL, ROWS = D // T, FF // T, E * CAP, T * CAP
    shapes = ((TOK, D), (1, DT, FF), (1, DT, FF), (1, FT, D))
    vm = pl.BlockSpec(memory_space=pltpu.VMEM)
    hb = pl.BlockSpec(memory_space=pl.ANY)
    dma = pltpu.SemaphoreType.DMA
    outs = pl.pallas_call(
        functools.partial(body, (E, T, CAP, TOK, D, FF)),
        name="routed_backward",
        out_shape=tuple(pltpu.VMEM(s, BF) for s in shapes),
        in_specs=[hb] * 7,
        out_specs=(vm, vm, vm, vm),
        scratch_shapes=[
            pltpu.VMEM((2, TOK), jnp.int32),
            pltpu.VMEM((2, TOK), F32),
            pltpu.VMEM((T * TOK, DT), BF),
            pltpu.VMEM((T * TOK, DT), BF),
            pltpu.VMEM((T, DT, FF), BF),
            pltpu.VMEM((T, DT, FF), BF),
            pltpu.VMEM((T, FT, D), BF),
            pltpu.VMEM((E * ROWS, T * TOK), BF),
            pltpu.VMEM((E, 2 * ROWS, DT), BF),
            pltpu.VMEM((E, 2 * ROWS, DT), BF),
            pltpu.VMEM((T, SL, 2 * DT), BF),
            pltpu.VMEM((SL, 3 * FF), BF),
            pltpu.VMEM((E, ROWS, DT), BF),
            pltpu.VMEM((E, ROWS, DT), BF),
            pltpu.VMEM((T, SL, 2 * DT), BF),
            pltpu.VMEM((T, SL, 3 * FF), BF),
            pltpu.VMEM((T, FT, DT), BF),
            pltpu.SemaphoreType.REGULAR((E // 4,)), pltpu.SemaphoreType.REGULAR((E // 4,)),
            dma((2 * T + 5,)),
            dma((E,)), dma((E,)),
            dma((3, 4)), dma((3, 4)),
            dma((E,)), dma((E,)),
            dma((2, T)), dma((2, T)),
            dma((2, T)), dma((2, T)),
            dma((T,)), dma((T,)),
        ],
        compiler_params=pltpu.CompilerParams(
            collective_id=0, has_side_effects=True, vmem_limit_bytes=56 << 20
        ),
    )(expert_ids.T, gate_wts.T, tokens, cotangent, w_gate, w_up, w_down)
    outs = [pltpu.with_memory_space_constraint(o, pltpu.VMEM) for o in outs]
    return pl.pallas_call(
        put,
        name="put",
        out_shape=tuple(jax.ShapeDtypeStruct(s, BF) for s in shapes),
        in_specs=[vm] * 4,
        out_specs=(hb,) * 4,
        scratch_shapes=[dma((4,))],
    )(*outs)


def solution(mesh):
    rows = P(("group", "expert", "tensor"), None)
    grads = P(("group", "expert"), "tensor", None)
    return jax.shard_map(
        local,
        mesh=mesh,
        in_specs=(rows, rows, rows, rows) + (P("expert", "tensor", None),) * 3,
        out_specs=(rows, grads, grads, grads),
        check_vma=False,
    )
```

time: 180 us -> 168 us (0.933); the launches traced: 180 us -> 166 us
  local copies, waits for them, and re-layouts: 7.2 us -> 0 us
  Pallas kernels: 172 us -> 165 us
    pallas_call x1, Pallas kernels: 172 us -> 164 us  [local(): pl.pallas_call(functools.partial(body, (E, T, CAP, TOK, D, FF)), name='ro...]
    unnamed x14 -> x0, local copies, waits for them, and re-layouts: 5.87 us -> none
where the time goes in v2:
time: 168 us; the launch traced here: 166 us
  Pallas kernels  165 us (98%)
    pallas_call x1, Pallas kernels, local(): pl.pallas_call(functools.partial(body, (E, T, CAP, TOK, D, FF)), name='ro...  164 us

profile of v2, /device:TPU:33, one launch (start us, length us, event | category | flops | bytes accessed | tf_op | source)
XLA Modules:
  0.0 165.7 jit_solution(12182786099277418910)
XLA Ops:
  0.6 163.7 %routed_backward.1 = (bf16[64,4096]{1,0:T(8,128)(2,1)S(1)}, bf16[1,1024,256]{2,1,0:T(8,128)(2,1)S(1)}, bf16[1,1024,256]{2,1,0:T(8,128)(2,1)S(1)}, bf16[1,64,4096]{2,1,0:T(8,128)(2,1)S(1)}) custom-call(s32[2,64]{1,0:T(2,128)} %bitcast.2, f32[2,64]{1,0:T(2,128)} %bitcast.3, bf16[64,4096]{1,0:T(8,128)(2,1)} %tok_hbm.1, bf16[64,4096]{1,0:T(8,128)(2,1)} %cot_hbm.1, ...), custom_call_target="tpu_custom_call" | custom-call | tf_op jit(solution)/shard_map/routed_backward/pallas_call | solution.py:380
  164.3 1.3 put.1

commit v3 on v2

--- a/solution.py
+++ b/solution.py
@@ -55,7 +55,7 @@
     near_by = [z * 2 + 1 - core, up * 2 + core, up * 2 + 1 - core, below * 2 + core, below * 2 + 1 - core]
     for e in near_by:
         pl.semaphore_signal(bar, 1, device_id={"expert": e}, device_id_type=MESH)
-    for k in range(1, T):
+    for k in (1, T - 1):
         pl.semaphore_signal(bar, 1, device_id={"tensor": side(k)}, device_id_type=MESH)
 
     def tell_up(k):
@@ -83,24 +83,24 @@
     W = T * TOK
     for c in head:
         c.wait()
-    ids = jnp.concatenate([idv[...]] * T, axis=1)
-    gts = jnp.concatenate([gtv[...]] * T, axis=1)
-    i0 = ids[0:1, :]
-    i1 = ids[1:2, :]
-    ex = iota((E, W), 0)
+    i0 = idv[0:1, :]
+    i1 = idv[1:2, :]
+    ex = iota((E, TOK), 0)
     h0 = i0 == ex
     h1 = i1 == ex
     both = (jnp.where(h0, 1.0, 0.0) + jnp.where(h1, 1.0, 0.0)).astype(BF)
-    ra = iota((W, W), 0)
-    rb = iota((W, W), 1)
-    before = jnp.where((ra // TOK == rb // TOK) & (ra < rb), 1.0, 0.0).astype(BF)
+    before = jnp.where(iota((TOK, TOK), 0) < iota((TOK, TOK), 1), 1.0, 0.0).astype(BF)
     count = dot(both, before)
     p0 = jnp.sum(jnp.where(h0, count, 0.0), axis=0, keepdims=True).astype(jnp.int32)
     p1 = jnp.sum(jnp.where(h1, count, 0.0), axis=0, keepdims=True).astype(jnp.int32)
-    s0 = jnp.where(p0 < CAP, i0 * CAP + p0, -1)
-    s1 = jnp.where(p1 < CAP, i1 * CAP + p1, -1)
-    g0 = gts[0:1, :]
-    g1 = gts[1:2, :]
+
+    def wide(v):
+        return jnp.concatenate([v] * T, axis=1)
+
+    s0 = wide(jnp.where(p0 < CAP, i0 * CAP + p0, -1))
+    s1 = wide(jnp.where(p1 < CAP, i1 * CAP + p1, -1))
+    g0 = wide(gtv[0:1, :])
+    g1 = wide(gtv[1:2, :])
 
     for c in loads[: 2 * T]:
         c.wait()
@@ -164,7 +164,7 @@
         )
 
     build(0)
-    pl.semaphore_wait(bar, len(near_by) + T - 1)
+    pl.semaphore_wait(bar, len(near_by) + 2)
     tell_below(1)
     tell_up(1)
     for j in range(1, EB):
@@ -231,9 +231,9 @@
             device_id={"expert": to}, device_id_type=MESH,
         )
 
-    def start_back(j, c):
-        back(j).start()
-        return c
+    def start_back(j, last):
+        back(last - j).start()
+        return last
 
     def expert(lo, hi):
         sl = pl.ds(lo * GS, (hi - lo) * GS)
@@ -256,7 +256,7 @@
             m = jnp.concatenate([p[o : o + GS] for p in parts], axis=0)
             v = dot(fold, m).astype(BF)
             rsend[pl.ds(g * GRP, GRP)] = v.reshape(GRP, ROWS, DT)
-        lax.fori_loop(max(1, lo * GRP), hi * GRP, start_back, 0)
+        lax.fori_loop(max(1, lo * GRP), hi * GRP, start_back, max(1, lo * GRP) + hi * GRP - 1)
 
     def part_of(h):
         return pl.ds(0, (NG - 1) * GS) if h == 0 else pl.ds((NG - 1) * GS, GS)
@@ -289,11 +289,12 @@
             pass_on(n, k).start()
     for g in range(2, NG - 1):
         unpack(g)
-    for k in (1, 3, 2):
-        rows_to(0, k).start()
+    rows_to(0, 1).start()
+    rows_to(0, 3).start()
     for n in range(3):
         for k in range(2):
             passed_on(n, k).wait_recv()
+    rows_to(0, 2).start()
     expert(0, NG - 1)
     for k in (1, 3, 2):
         act_to(0, k).start()
@@ -332,13 +333,6 @@
         back(j).wait_recv()
         return c
 
-    lax.fori_loop(1, E, wait_back, 0)
-    for n in range(DT // CB):
-        r = ret[:, :, n * CB : (n + 1) * CB].reshape(E * ROWS, CB)
-        v = dot(unpick, r).astype(BF)
-        for q in range(T):
-            ig_ref[:, q * DT + n * CB : q * DT + (n + 1) * CB] = v[q * TOK : (q + 1) * TOK]
-
     def drain(j, c):
         dispatch(j).wait_send()
         back(j).wait_send()
@@ -355,6 +349,12 @@
             act_to(h, k).wait_send()
         down_to(k).wait_send()
         down_to(k).wait_recv()
+    lax.fori_loop(1, E, wait_back, 0)
+    for n in range(DT // CB):
+        r = ret[:, :, n * CB : (n + 1) * CB].reshape(E * ROWS, CB)
+        v = dot(unpick, r).astype(BF)
+        for q in range(T):
+            ig_ref[:, q * DT + n * CB : q * DT + (n + 1) * CB] = v[q * TOK : (q + 1) * TOK]
 
 
 def put(*refs):

time: 168 us -> 165 us (0.982); the launches traced: 166 us -> 165 us
  no operation moved by 1% of the time
where the time goes in v3:
time: 165 us
  Pallas kernels  165 us (100%)
    pallas_call x1, Pallas kernels, local(): pl.pallas_call(functools.partial(body, (E, T, CAP, TOK, D, FF)), name='ro...  163 us

profile of v3, /device:TPU:33, one launch (start us, length us, event | category | flops | bytes accessed | tf_op | source)
XLA Modules:
  0.0 165.2 jit_solution(2767374816858962977)
XLA Ops:
  0.6 163.2 %routed_backward.1 = (bf16[64,4096]{1,0:T(8,128)(2,1)S(1)}, bf16[1,1024,256]{2,1,0:T(8,128)(2,1)S(1)}, bf16[1,1024,256]{2,1,0:T(8,128)(2,1)S(1)}, bf16[1,64,4096]{2,1,0:T(8,128)(2,1)S(1)}) custom-call(s32[2,64]{1,0:T(2,128)} %bitcast.2, f32[2,64]{1,0:T(2,128)} %bitcast.3, bf16[64,4096]{1,0:T(8,128)(2,1)} %tok_hbm.1, bf16[64,4096]{1,0:T(8,128)(2,1)} %cot_hbm.1, ...), custom_call_target="tpu_custom_call" | custom-call | tf_op jit(solution)/shard_map/routed_backward/pallas_call | solution.py:380
  163.8 1.3 put.1

commit v4 on v3

--- a/solution.py
+++ b/solution.py
@@ -23,8 +23,8 @@
 def body(
     sizes,
     ids_hbm, gts_hbm, tok_hbm, cot_hbm, wg_hbm, wu_hbm, wd_hbm,
-    ig_ref, gg_ref, gu_ref, gd_ref,
-    idv, gtv, tokv, cotv, wg, wu, wd, pick, send, recv, rc, gact, rsend, ret, xrc, xact, down,
+    ret, unpick, gg_ref, gu_ref, gd_ref,
+    idv, gtv, tokv, cotv, wg, wu, wd, pick, send, recv, rc, gact, rsend, xrc, xact, down,
     from_up, from_below, in_sem, ssem, rsem, wssem, wrsem, bssem, brsem, rcss, rcrs, actss, actrs, dss, drs,
 ):
     E, T, CAP, TOK, D, FF = sizes
@@ -327,7 +327,7 @@
         gg_ref[0, n * CB : (n + 1) * CB, :] = v[:, 0:FF]
         gu_ref[0, n * CB : (n + 1) * CB, :] = v[:, FF : 2 * FF]
 
-    unpick = pick[...].astype(F32).T.astype(BF)
+    unpick[...] = pick[...].astype(F32).T.astype(BF)
 
     def wait_back(j, c):
         back(j).wait_recv()
@@ -350,18 +350,25 @@
         down_to(k).wait_send()
         down_to(k).wait_recv()
     lax.fori_loop(1, E, wait_back, 0)
-    for n in range(DT // CB):
-        r = ret[:, :, n * CB : (n + 1) * CB].reshape(E * ROWS, CB)
-        v = dot(unpick, r).astype(BF)
-        for q in range(T):
-            ig_ref[:, q * DT + n * CB : q * DT + (n + 1) * CB] = v[q * TOK : (q + 1) * TOK]
-
-
-def put(*refs):
-    n = (len(refs) - 1) // 2
-    copies = [pltpu.make_async_copy(refs[i], refs[n + i], refs[-1].at[i]) for i in range(n)]
+
+
+def put(ret, unpick, gg, gu, gd, ig_out, gg_out, gu_out, gd_out, ig, sem):
+    copies = [
+        pltpu.make_async_copy(src, dst, sem.at[i])
+        for i, (src, dst) in enumerate(((gg, gg_out), (gu, gu_out), (gd, gd_out)))
+    ]
     for c in copies:
         c.start()
+    TOK, D = ig.shape
+    E, ROWS, DT = ret.shape
+    T = D // DT
+    for q in range(T):
+        v = dot(unpick[q * TOK : (q + 1) * TOK, :], ret[...].reshape(E * ROWS, DT)).astype(BF)
+        cols = pl.ds(q * DT, DT)
+        ig[:, cols] = v
+        c = pltpu.make_async_copy(ig.at[:, cols], ig_out.at[:, cols], sem.at[3 + q])
+        c.start()
+        copies.append(c)
     for c in copies:
         c.wait()
 
@@ -374,15 +381,16 @@
     CAP = 2 * TOK // E
     DT, FT, SL, ROWS = D // T, FF // T, E * CAP, T * CAP
     shapes = ((TOK, D), (1, DT, FF), (1, DT, FF), (1, FT, D))
+    inner = ((E, ROWS, DT), (T * TOK, E * ROWS)) + shapes[1:]
     vm = pl.BlockSpec(memory_space=pltpu.VMEM)
     hb = pl.BlockSpec(memory_space=pl.ANY)
     dma = pltpu.SemaphoreType.DMA
     outs = pl.pallas_call(
         functools.partial(body, (E, T, CAP, TOK, D, FF)),
         name="routed_backward",
-        out_shape=tuple(pltpu.VMEM(s, BF) for s in shapes),
+        out_shape=tuple(pltpu.VMEM(s, BF) for s in inner),
         in_specs=[hb] * 7,
-        out_specs=(vm, vm, vm, vm),
+        out_specs=(vm,) * 5,
         scratch_shapes=[
             pltpu.VMEM((2, TOK), jnp.int32),
             pltpu.VMEM((2, TOK), F32),
@@ -396,7 +404,6 @@
             pltpu.VMEM((E, 2 * ROWS, DT), BF),
             pltpu.VMEM((T, SL, 2 * DT), BF),
             pltpu.VMEM((SL, 3 * FF), BF),
-            pltpu.VMEM((E, ROWS, DT), BF),
             pltpu.VMEM((E, ROWS, DT), BF),
             pltpu.VMEM((T, SL, 2 * DT), BF),
             pltpu.VMEM((T, SL, 3 * FF), BF),
@@ -419,9 +426,9 @@
         put,
         name="put",
         out_shape=tuple(jax.ShapeDtypeStruct(s, BF) for s in shapes),
-        in_specs=[vm] * 4,
+        in_specs=[vm] * 5,
         out_specs=(hb,) * 4,
-        scratch_shapes=[dma((4,))],
+        scratch_shapes=[pltpu.VMEM((TOK, D), BF), dma((3 + T,))],
     )(*outs)
 
 

time: 165 us -> 165 us (level)
  no operation moved by 1% of the time
where the time goes in v4:
time: 165 us
  Pallas kernels  164 us (99%)
    pallas_call x1, Pallas kernels, local(): pl.pallas_call(functools.partial(body, (E, T, CAP, TOK, D, FF)), name='ro...  163 us

profile of v4, /device:TPU:33, one launch (start us, length us, event | category | flops | bytes accessed | tf_op | source)
XLA Modules:
  0.0 164.9 jit_solution(18133239830103875636)
XLA Ops:
  0.6 162.7 %routed_backward.1 = (bf16[32,16,1024]{2,1,0:T(8,128)(2,1)S(1)}, bf16[256,512]{1,0:T(8,128)(2,1)S(1)}, bf16[1,1024,256]{2,1,0:T(8,128)(2,1)S(1)}, bf16[1,1024,25...) custom-call(s32[2,64]{1,0:T(2,128)} %bitcast.2, f32[2,64]{1,0:T(2,128)} %bitcast.3, bf16[64,4096]{1,0:T(8,128)(2,1)} %tok_hbm.1, ...), custom_call_target="tpu_custom_call" | custom-call | tf_op jit(solution)/shard_map/routed_backward/pallas_call | solution.py:388
  163.4 1.6 put.1
